TPU v7x, 8 devices: a whole 2x2x1 slice. The times are simulated.
8 devices in a mesh: replica: 2 (over z, y), model: 4 (over x, core).
Axes of the slice: x: 2, y: 2, z: 1, core: 2. Of those that a mesh axis runs over, the one named last changes fastest.
Arguments:
- x: bfloat16 [512, 2048], P('replica'), parts along dimension 0
- w_query: bfloat16 [2048, 2048], P(None, 'model')
- w_key: bfloat16 [2048, 128], replicated
- w_value: bfloat16 [2048, 128], replicated
- w_out: bfloat16 [2048, 2048], P('model')
- k_cache: bfloat16 [512, 1, 4096, 128], P('replica'), parts along dimension 0
- v_cache: bfloat16 [512, 1, 4096, 128], P('replica'), parts along dimension 0
- lengths: int32 [512], P('replica'), parts along dimension 0
Outputs:
- output 1: bfloat16 [512, 2048], P('replica'), parts along dimension 0
- output 2: bfloat16 [512, 1, 128], P('replica'), parts along dimension 0
- output 3: bfloat16 [512, 1, 128], P('replica'), parts along dimension 0
There are 2 independent parts. A program takes and returns all parts, laid end to end along the dimension named above; an argument that names none is the same for every part.
All inputs are finite; a program needn't handle non-finite values.
Results may differ from a plain program's by a relative error of at most 0.00377298.
Values are sent between devices in bfloat16 or wider.
A program may use at most 2.25 GiB of HBM per device.

v0:
```python
import jax
import jax.numpy as jnp
from jax import lax
from jax.sharding import PartitionSpec as P


def attend(queries, k_rows, v_rows, k_one, v_one, seq_lens):
    inv_sqrt = queries.shape[-1] ** -0.5
    scores = jnp.einsum("bgrd,bgtd->bgrt", queries, k_rows, preferred_element_type=jnp.float32) * inv_sqrt
    score_new = jnp.einsum("bgrd,bgd->bgr", queries, k_one, preferred_element_type=jnp.float32) * inv_sqrt
    positions = jnp.arange(k_rows.shape[2])
    in_range = positions[None, None, None, :] < seq_lens[:, None, None, None]
    scores = jnp.where(in_range, scores, -jnp.inf)
    row_max = jnp.maximum(jnp.max(scores, axis=-1), score_new)
    weights = jnp.exp(scores - row_max[..., None])
    weight_new = jnp.exp(score_new - row_max)
    norm_sum = jnp.sum(weights, axis=-1) + weight_new
    out_sum = jnp.einsum("bgrt,bgtd->bgrd", weights.astype(jnp.bfloat16), v_rows, preferred_element_type=jnp.float32)
    out_sum = out_sum + weight_new.astype(jnp.bfloat16).astype(jnp.float32)[..., None] * v_one.astype(jnp.float32)[:, :, None, :]
    return (out_sum / norm_sum[..., None]).astype(jnp.bfloat16)


def solution(mesh):
    model_size = mesh.shape["model"]

    def local_step(x, w_query, w_key, w_value, w_out, k_cache, v_cache, lengths):
        batch_rows = x.shape[0]
        kv_heads = k_cache.shape[1]
        head_dim = k_cache.shape[3]
        local_rows = batch_rows // model_size
        row_start = lax.axis_index("model") * local_rows
        q_local = jnp.dot(x, w_query, preferred_element_type=jnp.float32).astype(jnp.bfloat16)
        q_rows = lax.all_to_all(q_local, "model", 0, 1, tiled=True)
        k_new = jnp.dot(x, w_key, preferred_element_type=jnp.float32).astype(jnp.bfloat16).reshape(batch_rows, kv_heads, head_dim)
        v_new = jnp.dot(x, w_value, preferred_element_type=jnp.float32).astype(jnp.bfloat16).reshape(batch_rows, kv_heads, head_dim)
        queries = q_rows.reshape(local_rows, kv_heads, -1, head_dim)
        out_rows = attend(
            queries,
            lax.dynamic_slice_in_dim(k_cache, row_start, local_rows, axis=0),
            lax.dynamic_slice_in_dim(v_cache, row_start, local_rows, axis=0),
            lax.dynamic_slice_in_dim(k_new, row_start, local_rows, axis=0),
            lax.dynamic_slice_in_dim(v_new, row_start, local_rows, axis=0),
            lax.dynamic_slice_in_dim(lengths, row_start, local_rows, axis=0),
        )
        out_heads = lax.all_to_all(out_rows.reshape(local_rows, -1), "model", 1, 0, tiled=True)
        part_sum = jnp.dot(out_heads, w_out, preferred_element_type=jnp.float32)
        full_sum = lax.psum(part_sum, "model")
        y = (x.astype(jnp.float32) + full_sum).astype(jnp.bfloat16)
        return y, k_new, v_new

    rows_spec = P("replica")
    return jax.shard_map(
        local_step,
        mesh=mesh,
        in_specs=(P("replica", None), P(None, "model"), P(), P(), P("model", None), rows_spec, rows_spec, rows_spec),
        out_specs=(rows_spec, rows_spec, rows_spec),
        check_vma=False,
    )
```

profile of v0, /device:TPU:0, one launch (start us, length us, event | category | flops | bytes accessed | tf_op | source)
XLA Modules:
  0.0 159.3 jit_solution(7079526925297099586)
XLA Ops:
  7.2 0.0 copy-start
  7.2 3.5 %convolution_convert_fusion = bf16[256,512]{1,0:T(8,128)(2,1)} fusion(bf16[256,2048]{1,0:T(8,128)(2,1)} %param.8, bf16[2048,512]{1,0:T(8,128)(2,1)} %param.9), kind=kOutput, calls=%fused_computation.17 | convolution fusion | flops 537001984 | bytes 3407872 | tf_op jit(solution)/shard_map/dot_general | solution.py:32
  10.6 4.6 %all-to-all-start = ((bf16[4,64,512]{2,1,0:T(8,128)(2,1)}), bf16[4,64,512]{2,1,0:T(8,128)(2,1)S(1)}, u32[]{:S(2)}, u32[]{:S(2)}) async-start(bf16[4,64,512]{2,1,0:T(8,128)(2,1)} %bitcast), calls=%async_computation | async-start | bytes 524288 | tf_op jit(solution)/shard_map/all_to_all | solution.py:33
  15.3 0.0 all-reduce.2.cloned.1.call-start
  15.3 1.8 %convolution_convert_fusion.2 = bf16[256,128]{1,0:T(8,128)(2,1)S(1)} fusion(bf16[256,2048]{1,0:T(8,128)(2,1)} %param.8, bf16[2048,128]{1,0:T(8,128)(2,1)} %param.10), kind=kOutput, calls=%fused_computation.19 | convolution fusion | flops 134250496 | bytes 1638400 | tf_op jit(solution)/shard_map/dot_general | solution.py:34
  17.0 0.0 copy-start.2
  17.1 1.8 %convolution_convert_fusion.1 = bf16[256,128]{1,0:T(8,128)(2,1)S(1)} fusion(bf16[256,2048]{1,0:T(8,128)(2,1)} %param.8, bf16[2048,128]{1,0:T(8,128)(2,1)} %param.11), kind=kOutput, calls=%fused_computation.18 | convolution fusion | flops 134250496 | bytes 1638400 | tf_op jit(solution)/shard_map/dot_general | solution.py:35
  18.9 0.0 copy-start.3
  18.9 0.8 dynamic_slice.11
  19.7 0.2 iota_compare_fusion
  19.9 1.1 all-to-all-done
  21.1 0.2 copy.12
  21.3 0.1 reshape.106
  21.4 0.2 fusion.29
  21.6 32.5 %fusion.6 = (f32[64,16]{1,0:T(8,128)S(1)}, f32[64,16,4096]{2,1,0:T(8,128)}) fusion(pred[64,4096]{1,0:T(8,128)(4,1)S(1)} %iota_compare_fusion, bf16[64,16,128]{2,1,0:T(8,128)(2,1)S(1)} %reshape.106, bf16[256,1,4096,128]{3,2,1,0:T(8,128)(2,1)} %param.13, s32[]{:T(128)S(6)} %select_n.12), kind=kOutput, calls=%fused_computation.8 | convolution fusion | flops 1086323712 | bytes 84414464 | tf_op jit(solution)/shard_map/bgrd,bgtd->bgrt/dot_general | solution.py:9
  54.1 8.3 %fusion.7 = f32[64,16]{1,0:T(8,128)S(1)} fusion(f32[64,16,4096]{2,1,0:T(8,128)} %get-tuple-element.6, f32[64,16]{1,0:T(8,128)S(1)} %multiply_maximum_fusion, pred[64,4096]{1,0:T(8,128)(4,1)S(1)} %iota_compare_fusion), kind=kLoop, calls=%fused_computation.9 | loop fusion | flops 16776192 | bytes 17047552 | tf_op jit(solution)/shard_map/reduce_sum | solution.py:17
  62.4 0.0 copy-start.1
  62.4 29.1 %fusion.24 = bf16[64,16,128]{2,1,0:T(8,128)(2,1)} fusion(bf16[256,1,4096,128]{3,2,1,0:T(8,128)(2,1)} %param.14, s32[]{:T(128)S(6)} %select_n.12, f32[64,16,4096]{2,1,0:T(8,128)} %get-tuple-element.6, f32[64,16]{1,0:T(8,128)S(1)} %multiply_maximum_fusion, pred[64,4096]{1,0:T(8,128)(4,1)S(1)} %iota_compare_fusion, f32[64,16]{1,0:T(8,128)S(1)} %get-tuple-element.4, ...), kind=kOutput, calls=%fused_computation.22 | convolution fusion | flops 1091043328 | bytes 84455424 | tf_op jit(solution)/shard_map/bgrt,bgtd->bgrd/dot_general | solution.py:18
  91.5 1.1 all_to_all.29
  92.6 8.4 %all_to_all.35 = bf16[64,4,512]{2,0,1:T(8,128)(2,1)S(1)} all-to-all(bf16[64,4,512]{2,0,1:T(8,128)(2,1)S(1)} %copy.13), channel_id=1, replica_groups=mesh['replica'=2,'model'=4] {'model'}, dimensions={1} | all-to-all | bytes 524288 | tf_op jit(solution)/shard_map/all_to_all | solution.py:45
  101.0 2.0 %fusion.36 = f32[256,2048]{1,0:T(8,128)} fusion(bf16[256,512]{1,0:T(8,128)(2,1)S(1)} %bitcast.35, bf16[512,2048]{1,0:T(8,128)(2,1)S(1)} %copy-done), kind=kOutput, calls=%fused_computation.35 | convolution fusion | flops 536870912 | bytes 4456448 | tf_op jit(solution)/shard_map/dot_general | solution.py:46
  103.1 0.0 all-reduce.2.cloned.1.call-update
  103.1 46.5 %all-reduce.2.cloned.1.call-done = f32[256,2048]{1,0:T(8,128)} async-done(((f32[256,2048]{1,0:T(8,128)}), f32[256,2048]{1,0:T(8,128)}) %all-reduce.2.cloned.1.call-update) | async-done | bytes 2097168 | tf_op jit(solution)/shard_map/psum | solution.py:47
  149.6 2.8 %add_convert_fusion = bf16[256,2048]{1,0:T(8,128)(2,1)} fusion(f32[256,2048]{1,0:T(8,128)} %all-reduce.2.cloned.1.call-done, bf16[256,2048]{1,0:T(8,128)(2,1)S(1)} %copy-done.1), kind=kLoop, calls=%fused_computation.15 | loop fusion | flops 1572864 | bytes 4194304 | tf_op jit(solution)/shard_map/convert_element_type | solution.py:48
  (9 shorter events, 0.1 us)
Async XLA Ops:
  7.2 93.9 %copy-start = (bf16[512,2048]{1,0:T(8,128)(2,1)S(1)}, bf16[512,2048]{1,0:T(8,128)(2,1)}, u32[]{:S(2)}) copy-start(bf16[512,2048]{1,0:T(8,128)(2,1)} %param.12) | copy-start | bytes 6291460
  10.6 10.4 %all-to-all-start = ((bf16[4,64,512]{2,1,0:T(8,128)(2,1)}), bf16[4,64,512]{2,1,0:T(8,128)(2,1)S(1)}, u32[]{:S(2)}, u32[]{:S(2)}) async-start(bf16[4,64,512]{2,1,0:T(8,128)(2,1)} %bitcast), calls=%async_computation | async-start | bytes 524288 | tf_op jit(solution)/shard_map/all_to_all | solution.py:33
  15.3 134.3 %all-reduce.2.cloned.1.call-start = ((), (), s32[]{:S(2)}) async-start(), calls=%async_computation.2 | async-start | bytes 4194304 | tf_op jit(solution)/shard_map/psum | solution.py:47
  17.0 4.0 %copy-start.2 = (bf16[256,128]{1,0:T(8,128)(2,1)}, bf16[256,128]{1,0:T(8,128)(2,1)S(1)}, u32[]{:S(2)}) copy-start(bf16[256,128]{1,0:T(8,128)(2,1)S(1)} %convolution_convert_fusion.2) | copy-start | bytes 196612
  18.9 2.2 %copy-start.3 = (bf16[256,128]{1,0:T(8,128)(2,1)}, bf16[256,128]{1,0:T(8,128)(2,1)S(1)}, u32[]{:S(2)}) copy-start(bf16[256,128]{1,0:T(8,128)(2,1)S(1)} %convolution_convert_fusion.1) | copy-start | bytes 196612
  62.4 87.1 %copy-start.1 = (bf16[256,2048]{1,0:T(8,128)(2,1)S(1)}, bf16[256,2048]{1,0:T(8,128)(2,1)}, u32[]{:S(2)}) copy-start(bf16[256,2048]{1,0:T(8,128)(2,1)} %param.8) | copy-start | bytes 3145732
Sparse Core Ops, SparseCore 0:
  103.2 46.3 all-reduce.1
where the time goes:
time: 160 us; the launch traced here: 159 us
  matrix products  70.9 us (44%)
  waiting for transfers between devices  47.6 us (30%)
  between operations  14.1 us (9%)
  other arithmetic  11.3 us (7%)
  blocking collectives  8.39 us (5%)
  starting transfers between devices  4.61 us (3%)
  local copies, waits for them, and re-layouts  2.23 us (1%)
    psum x1, waiting for transfers between devices, local_step(): full_sum = lax.psum(part_sum, 'model')  46.5 us
    dot_general x1, matrix products, attend(): jnp.einsum('bgrd,bgtd->bgrt', queries, k_rows, preferred_element_type=jnp...  32.5 us
    dot_general x1, matrix products, attend(): jnp.einsum('bgrt,bgtd->bgrd', weights.astype(jnp.bfloat16), v_rows, prefe...  29.1 us
    all_to_all x1, blocking collectives, local_step(): lax.all_to_all(out_rows.reshape(local_rows, -1), 'model', 1, 0, tiled=True)  8.39 us
    reduce_sum x1, other arithmetic, attend(): norm_sum = jnp.sum(weights, axis=-1) + weight_new  8.25 us
    all_to_all x1, starting transfers between devices, local_step(): q_rows = lax.all_to_all(q_local, 'model', 0, 1, tiled=True)  4.61 us
    dot_general x1, matrix products, local_step(): jnp.dot(x, w_query, preferred_element_type=jnp.float32).astype(jnp.bfloat16)  3.47 us
  transfers between devices with their start and end apart: 2, of which 2 were waited for; matrix products, arithmetic and copies ran while one was open for 3% of the time, Pallas kernels for 0%

commit v1 on v0

v1 whole, which is shorter than its diff:
```python
import functools

import jax
import jax.numpy as jnp
from jax import lax
from jax.experimental import pallas as pl
from jax.experimental.pallas import tpu as pltpu
from jax.sharding import PartitionSpec as P

MESH = pl.DeviceIdType.MESH
F32 = jnp.float32
BF16 = jnp.bfloat16
NEG = float("-inf")

BATCH = 256
HALF = 128
DIM = 128
LONG_ROWS = 32
SHORT_ROWS = HALF - LONG_ROWS
FIRST = 32
BLOCK = 512


def nt_dot(a, b):
    return lax.dot_general(a, b, (((1,), (1,)), ((), ())), preferred_element_type=F32)


def dot(a, b):
    return jnp.dot(a, b, preferred_element_type=F32)


def order_tables(lens_row):
    i_sub = lax.broadcasted_iota(jnp.int32, (BATCH, BATCH), 0)
    i_lane = lax.broadcasted_iota(jnp.int32, (BATCH, BATCH), 1)
    row = jnp.broadcast_to(lens_row, (BATCH, BATCH))
    col = jnp.sum(jnp.where(i_sub == i_lane, row, 0.0), axis=1, keepdims=True)
    ahead = (col > row) | ((col == row) & (i_sub < i_lane))
    ahead = jnp.where(ahead, 1.0, 0.0)
    rank_row = jnp.sum(ahead, axis=0, keepdims=True).astype(jnp.int32)
    rank_col = (BATCH - 1) - jnp.sum(ahead, axis=1, keepdims=True).astype(jnp.int32)

    def place(rank):
        slot = rank >> 1
        return ((rank + slot) & 1) * HALF + slot

    return place(rank_row), place(rank_col), col


def project_kernel(x_hbm, wq_hbm, wk_hbm, wv_hbm, lens_ref,
                   q_out, kn_out, vn_out, kp_out, vp_out, meta_out, lenc_out, perm_out, back_out,
                   xv, wqv, wkv, qv, send_buf, sems, ssem, rsem):
    m = lax.axis_index("model")
    r = lax.axis_index("replica")
    core = m % 2
    sib = m + 1 - 2 * core
    depth = x_hbm.shape[1]
    parts = 4
    step = depth // parts
    loads = []
    for i in range(parts):
        cut = pl.ds(i * step, step)
        a = pltpu.make_async_copy(x_hbm.at[:, cut], xv.at[:, cut], sems.at[2 * i])
        b = pltpu.make_async_copy(wq_hbm.at[cut, :], wqv.at[cut, :], sems.at[2 * i + 1])
        a.start()
        b.start()
        loads.append((a, b))
    lk = pltpu.make_async_copy(wk_hbm, wkv.at[:, pl.ds(0, DIM)], sems.at[2 * parts])
    lv = pltpu.make_async_copy(wv_hbm, wkv.at[:, pl.ds(DIM, DIM)], sems.at[2 * parts + 1])
    lk.start()
    lv.start()
    barrier = pltpu.get_barrier_semaphore()
    pl.semaphore_signal(barrier, inc=1, device_id=(r, sib), device_id_type=MESH)
    pl.semaphore_wait(barrier, 1)

    pos_row, pos_col, len_col = order_tables(lens_ref[...].astype(F32))
    p_iota = lax.broadcasted_iota(jnp.int32, (HALF, BATCH), 0)
    own = jnp.where(p_iota + core * HALF == pos_row, 1.0, 0.0)
    own_bf = own.astype(BF16)
    oth_bf = jnp.where(p_iota + (1 - core) * HALF == pos_row, 1.0, 0.0).astype(BF16)
    perm_out[...] = jnp.where(
        lax.broadcasted_iota(jnp.int32, (BATCH, BATCH), 0) == pos_row, 1.0, 0.0).astype(BF16)
    back_out[...] = jnp.where(
        lax.broadcasted_iota(jnp.int32, (BATCH, BATCH), 1) == pos_col, 1.0, 0.0).astype(BF16)
    own_t = lax.broadcasted_iota(jnp.int32, (BATCH, HALF), 1) + core * HALF == pos_col
    i_col = lax.broadcasted_iota(jnp.int32, (BATCH, HALF), 0).astype(F32)
    meta_out[...] = jnp.zeros_like(meta_out)
    meta_out[0:1, :] = jnp.sum(jnp.where(own_t, i_col, 0.0), axis=0, keepdims=True).astype(jnp.int32)
    meta_out[1:2, :] = jnp.sum(jnp.where(own_t, len_col, 0.0), axis=0, keepdims=True).astype(jnp.int32)
    own_len = jnp.sum(own * lens_ref[...].astype(F32), axis=1, keepdims=True)
    lenc_out[...] = jnp.broadcast_to(own_len, (HALF, DIM)).astype(jnp.int32)

    acc = None
    for i in range(parts):
        loads[i][0].wait()
        loads[i][1].wait()
        cut = pl.ds(i * step, step)
        t = dot(xv[:, cut], wqv[cut, :])
        acc = t if acc is None else acc + t
    qv[...] = acc.astype(BF16)
    q_oth = dot(oth_bf, qv[...]).astype(BF16)
    for h in range(4):
        send_buf[h] = q_oth[:, h * DIM:(h + 1) * DIM]
    push = pltpu.make_async_remote_copy(
        src_ref=send_buf, dst_ref=q_out.at[pl.ds(4, 4)], send_sem=ssem, recv_sem=rsem,
        device_id=(r, sib), device_id_type=MESH)
    push.start()
    q_own = dot(own_bf, qv[...]).astype(BF16)
    for h in range(4):
        q_out[h] = q_own[:, h * DIM:(h + 1) * DIM]
    lk.wait()
    lv.wait()
    kv = dot(xv[...], wkv[...]).astype(BF16)
    kn_out[...] = kv[:, :DIM]
    vn_out[...] = kv[:, DIM:]
    kv_own = dot(own_bf, kv)
    kp_out[...] = kv_own[:, :DIM]
    vp_out[...] = kv_own[:, DIM:]
    push.wait()


def attend_kernel(j0, rows, slots, meta, q_ref, kp, vp, lenc, kc, vc, w_own, w_sib, _order,
                  mine_out, send_out,
                  qf, kfirst, vfirst, kb, vb, wv, osc, asem, bsem, wsem):
    m = lax.axis_index("model")
    chip = m // 2
    scale = DIM ** -0.5

    def first_copies(j, _):
        src = meta[0, j0 + j]
        at = pl.ds(pl.multiple_of(j * FIRST, FIRST), FIRST)
        pltpu.make_async_copy(kc.at[src, 0, pl.ds(0, FIRST), :], kfirst.at[at, :], asem.at[0]).start()
        pltpu.make_async_copy(vc.at[src, 0, pl.ds(0, FIRST), :], vfirst.at[at, :], asem.at[1]).start()
        return 0

    lax.fori_loop(0, rows, first_copies, 0)

    def blocks_of(j):
        return (meta[1, j0 + j] + (BLOCK - 1)) // BLOCK

    def issue(j):
        src = meta[0, j0 + j]
        slot = j % slots

        def one(cache, buf, sem):
            def go(b, _):
                at = pl.ds(pl.multiple_of(b * BLOCK, BLOCK), BLOCK)
                pltpu.make_async_copy(cache.at[src, 0, at, :], buf.at[slot, at, :], sem).start()
                return 0
            lax.fori_loop(0, blocks_of(j), go, 0)

        one(kc, kb, bsem.at[0, slot])
        one(vc, vb, bsem.at[1, slot])

    n_long = lax.fori_loop(
        0, rows, lambda j, n: n + jnp.where(meta[1, j0 + j] > FIRST, 1, 0), jnp.int32(0))

    def prime(j, _):
        issue(j)
        return 0

    lax.fori_loop(0, jnp.minimum(n_long, slots), prime, 0)
    wo = pltpu.make_async_copy(w_own, wv.at[pl.ds(0, 512), :], wsem.at[0])
    ws = pltpu.make_async_copy(w_sib, wv.at[pl.ds(512, 512), :], wsem.at[1])
    wo.start()
    ws.start()

    for h in range(8):
        qf[h * HALF:(h + 1) * HALF, :] = q_ref[h].astype(F32)

    pltpu.make_async_copy(kfirst, kfirst, asem.at[0]).wait()
    pltpu.make_async_copy(vfirst, vfirst, asem.at[1]).wait()
    lane = lax.broadcasted_iota(jnp.int32, (64, 256), 1)
    sub = lax.broadcasted_iota(jnp.int32, (64, 256), 0)
    same = (lane // FIRST) == (sub % 8)
    tok = lane % FIRST
    for g in range(rows // 8):
        a = j0 + g * 8
        q = jnp.concatenate([qf[h * HALF + a:h * HALF + a + 8, :] for h in range(8)], axis=0)
        kn = jnp.concatenate([kp[a:a + 8, :]] * 8, axis=0)
        vn = jnp.concatenate([vp[a:a + 8, :]] * 8, axis=0)
        ln = jnp.concatenate([jnp.concatenate([lenc[a:a + 8, :]] * 8, axis=0)] * 2, axis=1)
        at = slice(g * 256, (g + 1) * 256)
        s = nt_dot(q.astype(BF16), kfirst[at, :]) * scale
        s = jnp.where(same & (tok < ln), s, NEG)
        sn = jnp.sum(q * kn, axis=1, keepdims=True) * scale
        top = jnp.maximum(jnp.max(s, axis=1, keepdims=True), sn)
        e = jnp.exp(s - top)
        en = jnp.exp(sn - top)
        tot = jnp.sum(e, axis=1, keepdims=True) + en
        num = dot(e.astype(BF16), vfirst[at, :]) + en.astype(BF16).astype(F32) * vn
        o = num / tot
        for h in range(8):
            osc[h * rows + g * 8:h * rows + g * 8 + 8, :] = o[h * 8:(h + 1) * 8, :]

    def row_body(j, slot, length, n):
        q8 = qf[pl.ds(j0 + j, 8, stride=HALF), :]
        zero = jnp.zeros_like(q8)
        qq = jnp.concatenate(
            [jnp.concatenate([q8, zero], axis=1), jnp.concatenate([zero, q8], axis=1)], axis=0).astype(BF16)
        kn = kp[pl.ds(j0 + j, 1), :]
        vn = vp[pl.ds(j0 + j, 1), :]
        sn = jnp.sum(q8 * kn, axis=1, keepdims=True) * scale
        lane = lax.broadcasted_iota(jnp.int32, (16, BLOCK), 1)
        sub = lax.broadcasted_iota(jnp.int32, (16, BLOCK), 0)
        tok = lane + jnp.where(sub >= 8, BLOCK, 0)
        scores = []
        for b in range(n):
            at = 2 * b * BLOCK
            k2 = jnp.concatenate([kb[slot, at:at + BLOCK, :], kb[slot, at + BLOCK:at + 2 * BLOCK, :]], axis=1)
            s = nt_dot(qq, k2) * scale
            scores.append(jnp.where(tok + at < length, s, NEG))
        top = functools.reduce(jnp.maximum, scores)
        top = jnp.max(top, axis=1, keepdims=True)
        top = jnp.maximum(jnp.maximum(top[:8], top[8:]), sn)
        top2 = jnp.concatenate([top, top], axis=0)
        es = [jnp.exp(s - top2) for s in scores]
        tot = jnp.sum(functools.reduce(jnp.add, es), axis=1, keepdims=True)
        num = None
        for b in range(n):
            at = 2 * b * BLOCK
            v2 = jnp.concatenate([vb[slot, at:at + BLOCK, :], vb[slot, at + BLOCK:at + 2 * BLOCK, :]], axis=1)
            t = dot(es[b].astype(BF16), v2)
            num = t if num is None else num + t
        en = jnp.exp(sn - top)
        num = num[:8, :DIM] + num[8:, DIM:] + en.astype(BF16).astype(F32) * vn
        tot = tot[:8] + tot[8:] + en
        osc[pl.ds(j, 8, stride=rows), :] = num / tot

    def long_row(j, _):
        slot = j % slots
        length = meta[1, j0 + j]
        nb = blocks_of(j)

        def done(cache, buf, sem):
            def go(b, _):
                at = pl.ds(0, BLOCK)
                pltpu.make_async_copy(cache.at[0, 0, at, :], buf.at[slot, at, :], sem).wait()
                return 0
            lax.fori_loop(0, nb, go, 0)

        done(kc, kb, bsem.at[0, slot])
        done(vc, vb, bsem.at[1, slot])

        @pl.when(nb % 2 == 1)
        def _():
            at = pl.ds(pl.multiple_of(nb * BLOCK, BLOCK), BLOCK)
            kb[slot, at, :] = jnp.zeros((BLOCK, DIM), BF16)
            vb[slot, at, :] = jnp.zeros((BLOCK, DIM), BF16)

        pairs = (nb + 1) // 2
        for n in range(1, 5):
            @pl.when(pairs == n)
            def _(n=n):
                row_body(j, slot, length, n)

        @pl.when(j + slots < n_long)
        def _():
            issue(j + slots)
        return 0

    lax.fori_loop(0, n_long, long_row, 0)

    wo.wait()
    ws.wait()
    part = rows // 2

    def halves(h, which):
        return osc[pl.ds(h * rows + which * part, part), :]

    o = jnp.concatenate(
        [jnp.concatenate([halves(h, chip), halves(h, 1 - chip)], axis=0) for h in range(8)],
        axis=1).astype(BF16)
    for c in range(4):
        cut = slice(c * 512, (c + 1) * 512)
        res = dot(o, wv[:, cut])
        mine_out[:, cut] = res[:part]
        send_out[:, cut] = res[part:]


def combine_kernel(p1, r1, p2, s2, x_ref, perm, y, r2, ssem, rsem):
    m = lax.axis_index("model")
    r = lax.axis_index("replica")
    chip = m // 2
    core = m % 2
    sib = m + 1 - 2 * core
    far = (m + 2) % 4
    barrier = pltpu.get_barrier_semaphore()
    for other in (sib, far):
        pl.semaphore_signal(barrier, inc=1, device_id=(r, other), device_id_type=MESH)
    pl.semaphore_wait(barrier, 2)

    def place(which, f, c=core):
        n = (SHORT_ROWS if which == 0 else LONG_ROWS) // 2
        base = (LONG_ROWS if which == 0 else 0)
        return pl.ds(pl.multiple_of(c * HALF + base + f * n, 16), n)

    def push(src, dst, i, dev):
        c = pltpu.make_async_remote_copy(
            src_ref=src, dst_ref=dst, send_sem=ssem.at[i], recv_sem=rsem.at[i],
            device_id=(r, dev), device_id_type=MESH)
        c.start()
        return c

    sends = [push(s2, r2, 0, far)]

    def finish(which, mine, got):
        at = place(which, chip)
        xs = dot(perm[at, :], x_ref[...])
        y[at, :] = (xs + (mine + got)).astype(BF16)

    finish(0, p1[...], r1[...])
    mine1 = place(0, chip)
    far1 = push(y.at[mine1, :], y.at[mine1, :], 1, far)
    sib1 = push(y.at[mine1, :], y.at[mine1, :], 2, sib)
    sends[0].wait_recv()
    finish(1, p2[...], r2[...])
    mine2 = place(1, chip)
    far2 = push(y.at[mine2, :], y.at[mine2, :], 3, far)
    sib2 = push(y.at[mine2, :], y.at[mine2, :], 4, sib)
    far1.wait_recv()
    got1 = place(0, 1 - chip)
    fwd1 = push(y.at[got1, :], y.at[got1, :], 5, sib)
    far2.wait_recv()
    got2 = place(1, 1 - chip)
    fwd2 = push(y.at[got2, :], y.at[got2, :], 6, sib)
    for c in (sib1, sib2, fwd1, fwd2):
        c.wait_recv()
    for c in (sends[0], far1, sib1, far2, sib2, fwd1, fwd2):
        c.wait_send()


def cost(us):
    return pl.CostEstimate(flops=int(us * 3e8), bytes_accessed=int(us * 2e6), transcendentals=0)


VM = pl.BlockSpec(memory_space=pltpu.VMEM)
SM = pl.BlockSpec(memory_space=pltpu.SMEM)
ANY = pl.BlockSpec(memory_space=pl.ANY)


def sds(shape, dtype):
    return jax.ShapeDtypeStruct(shape, dtype)


def attend_call(j0, rows, slots, us, *args):
    part = rows // 2
    return pl.pallas_call(
        functools.partial(attend_kernel, j0, rows, slots),
        out_shape=(sds((part, 2048), F32), sds((part, 2048), F32)),
        in_specs=[SM, VM, VM, VM, VM, ANY, ANY, ANY, ANY, ANY],
        out_specs=(VM, VM),
        scratch_shapes=[
            pltpu.VMEM((8 * HALF, DIM), F32),
            pltpu.VMEM((rows * FIRST, DIM), BF16),
            pltpu.VMEM((rows * FIRST, DIM), BF16),
            pltpu.VMEM((slots, 4096, DIM), BF16),
            pltpu.VMEM((slots, 4096, DIM), BF16),
            pltpu.VMEM((1024, 2048), BF16),
            pltpu.VMEM((8 * rows, DIM), F32),
            pltpu.SemaphoreType.DMA((2,)),
            pltpu.SemaphoreType.DMA((2, slots)),
            pltpu.SemaphoreType.DMA((2,)),
        ],
        compiler_params=pltpu.CompilerParams(vmem_limit_bytes=32 * 1024 * 1024),
        cost_estimate=cost(us),
        name=f"attend_{j0}",
    )(*args)


def local_step(x, w_query, w_key, w_value, w_out, k_cache, v_cache, lengths):
    swap = [(i, i ^ 1) for i in range(4)]
    cross = [(i, i ^ 2) for i in range(4)]
    w_sib = lax.ppermute(w_out, "model", swap)
    q, k_new, v_new, kp, vp, meta, lenc, perm, back = pl.pallas_call(
        project_kernel,
        out_shape=(
            sds((8, HALF, DIM), BF16), sds((BATCH, DIM), BF16), sds((BATCH, DIM), BF16),
            sds((HALF, DIM), F32), sds((HALF, DIM), F32), sds((8, HALF), jnp.int32),
            sds((HALF, DIM), jnp.int32), sds((BATCH, BATCH), BF16), sds((BATCH, BATCH), BF16),
        ),
        in_specs=[ANY, ANY, ANY, ANY, VM],
        out_specs=(VM,) * 9,
        scratch_shapes=[
            pltpu.VMEM((BATCH, 2048), BF16),
            pltpu.VMEM((2048, 512), BF16),
            pltpu.VMEM((2048, 2 * DIM), BF16),
            pltpu.VMEM((BATCH, 512), BF16),
            pltpu.VMEM((4, HALF, DIM), BF16),
            pltpu.SemaphoreType.DMA((10,)),
            pltpu.SemaphoreType.DMA,
            pltpu.SemaphoreType.DMA,
        ],
        compiler_params=pltpu.CompilerParams(
            collective_id=0, has_side_effects=True, vmem_limit_bytes=24 * 1024 * 1024),
        cost_estimate=cost(5),
        name="project",
    )(x, w_query, w_key, w_value, lengths.reshape(1, BATCH))
    common = (meta, q, kp, vp, lenc, k_cache, v_cache, w_out, w_sib)
    p1, s1 = attend_call(LONG_ROWS, SHORT_ROWS, 2, 4, *common, meta)
    r1 = lax.ppermute(s1, "model", cross)
    p2, s2 = attend_call(0, LONG_ROWS, 6, 10, *common, p1)
    y_sorted = pl.pallas_call(
        combine_kernel,
        out_shape=sds((BATCH, 2048), BF16),
        in_specs=[VM] * 6,
        out_specs=VM,
        scratch_shapes=[
            pltpu.VMEM((LONG_ROWS // 2, 2048), F32),
            pltpu.SemaphoreType.DMA((7,)),
            pltpu.SemaphoreType.DMA((7,)),
        ],
        compiler_params=pltpu.CompilerParams(
            collective_id=1, has_side_effects=True, vmem_limit_bytes=24 * 1024 * 1024),
        cost_estimate=cost(10),
        name="combine",
    )(p1, r1, p2, s2, x, perm)
    y = jnp.dot(back, y_sorted, preferred_element_type=F32).astype(BF16)
    return y, k_new.reshape(BATCH, 1, DIM), v_new.reshape(BATCH, 1, DIM)


def solution(mesh):
    rows_spec = P("replica")
    return jax.shard_map(
        local_step,
        mesh=mesh,
        in_specs=(P("replica", None), P(None, "model"), P(), P(), P("model", None), rows_spec, rows_spec, rows_spec),
        out_specs=(rows_spec, rows_spec, rows_spec),
        check_vma=False,
    )
```

time: 160 us -> 49.3 us (0.31)
  matrix products: 70.9 us -> 1.41 us
  waiting for transfers between devices: 47.6 us -> 0.01 us
  Pallas kernels: 0 us -> 35.9 us
  between operations: 14.1 us -> 0.7 us
  other arithmetic: 11.3 us -> 0 us
  blocking collectives: 8.39 us -> 0 us
  local copies, waits for them, and re-layouts: 2.23 us -> 6.84 us
    dot_general x7 -> x1, matrix products: 70.9 us -> 1.41 us  [local_step(): y = jnp.dot(back, y_sorted, preferred_element_type=F32).astype(BF16)]
    psum x1 -> x0, waiting for transfers between devices: 46.5 us -> none  [local_step(): full_sum = lax.psum(part_sum, 'model')]
    pallas_call x0 -> x4, Pallas kernels: none -> 35.9 us  [the longest x2 20.7 us: attend_call(): pl.pallas_call(functools.partial(attend_kernel, j0, rows, slots), out_sha...]
    all_to_all x1 -> x0, blocking collectives: 8.39 us -> none  [local_step(): lax.all_to_all(out_rows.reshape(local_rows, -1), 'model', 1, 0, tiled=True)]
    reduce_sum x1 -> x0, other arithmetic: 8.25 us -> none  [attend(): norm_sum = jnp.sum(weights, axis=-1) + weight_new]
    unnamed x8 -> x16, local copies, waits for them, and re-layouts: 0.03 us -> 6.84 us
    all_to_all x1 -> x0, starting transfers between devices: 4.61 us -> none  [local_step(): q_rows = lax.all_to_all(q_local, 'model', 0, 1, tiled=True)]
    ppermute x0 -> x2, starting transfers between devices: none -> 3.54 us  [the longest x1 2.66 us: local_step(): r1 = lax.ppermute(s1, 'model', cross)]
  transfers between devices with their start and end apart: 2 -> 2, of which waited for: 2 -> 0; matrix products, arithmetic and copies ran while one was open for 3% -> 0% of each run, Pallas kernels for 0% -> 35%
where the time goes in v1:
time: 49.3 us; the launch traced here: 48.4 us
  Pallas kernels  35.9 us (73%)
  local copies, waits for them, and re-layouts  6.84 us (14%)
  starting transfers between devices  3.54 us (7%)
  matrix products  1.41 us (3%)
  between operations  0.7 us (1%)
    pallas_call x2, Pallas kernels, attend_call(): pl.pallas_call(functools.partial(attend_kernel, j0, rows, slots), out_sha...  20.7 us
    pallas_call x1, Pallas kernels, local_step(): pl.pallas_call(combine_kernel, out_shape=sds((BATCH, 2048), BF16), in_spe...  11.9 us
    unnamed x16, local copies, waits for them, and re-layouts  6.84 us
    pallas_call x1, Pallas kernels, local_step(): pl.pallas_call(project_kernel, out_shape=(sds((8, HALF, DIM), BF16), sds(...  3.42 us
    ppermute x1, starting transfers between devices, local_step(): r1 = lax.ppermute(s1, 'model', cross)  2.66 us
    dot_general x1, matrix products, local_step(): y = jnp.dot(back, y_sorted, preferred_element_type=F32).astype(BF16)  1.41 us
  transfers between devices with their start and end apart: 2, of which 0 were waited for; matrix products, arithmetic and copies ran while one was open for 0% of the time, Pallas kernels for 35%

profile of v1, /device:TPU:0, one launch (start us, length us, event | category | flops | bytes accessed | tf_op | source)
XLA Modules:
  0.0 48.4 jit_solution(1993584543938399400)
XLA Ops:
  0.6 0.9 %collective-permute-start = (bf16[512,2048]{1,0:T(8,128)(2,1)}, bf16[512,2048]{1,0:T(8,128)(2,1)S(1)}, u32[]{:S(2)}, u32[]{:S(2)}) collective-permute-start(bf16[512,2048]{1,0:T(8,128)(2,1)} %w_own.3), channel_id=1, source_target_pairs={{0,1},{1,0},{2,3},{3,2},{4,5},{5,4},{6,7},{7,6}} | collective-permute-start | bytes 6291464 | tf_op jit(solution)/shard_map/ppermute | solution.py:373
  1.5 0.0 copy-start.1
  1.5 1.6 %copy-done.1 = bf16[2048,512]{1,0:T(8,128)(2,1)S(1)} copy-done((bf16[2048,512]{1,0:T(8,128)(2,1)S(1)}, bf16[2048,512]{1,0:T(8,128)(2,1)}, u32[]{:S(2)}) %copy-start.1) | copy-done | bytes 2097176
  3.1 0.0 copy-start.2
  3.1 1.2 %copy-done.2 = bf16[256,2048]{1,0:T(8,128)(2,1)S(1)} copy-done((bf16[256,2048]{1,0:T(8,128)(2,1)S(1)}, bf16[256,2048]{1,0:T(8,128)(2,1)}, u32[]{:S(2)}) %copy-start.2) | copy-done | bytes 1048600
  4.3 0.0 copy-start.4
  4.3 1.0 %copy-done.4 = bf16[2048,128]{1,0:T(8,128)(2,1)S(1)} copy-done((bf16[2048,128]{1,0:T(8,128)(2,1)S(1)}, bf16[2048,128]{1,0:T(8,128)(2,1)}, u32[]{:S(2)}) %copy-start.4) | copy-done | bytes 524312
  5.4 0.0 copy-start.5
  5.4 1.0 %copy-done.5 = bf16[2048,128]{1,0:T(8,128)(2,1)S(1)} copy-done((bf16[2048,128]{1,0:T(8,128)(2,1)S(1)}, bf16[2048,128]{1,0:T(8,128)(2,1)}, u32[]{:S(2)}) %copy-start.5) | copy-done | bytes 524312
  6.4 0.0 copy-start.6
  6.4 0.7 %copy-done.6 = s32[256]{0:T(256)S(1)} copy-done((s32[256]{0:T(256)S(1)}, s32[256]{0:T(256)}, u32[]{:S(2)}) %copy-start.6) | copy-done | bytes 1048
  7.1 0.0 copy-start
  7.1 3.4 %project.1 = (bf16[8,128,128]{2,1,0:T(8,128)(2,1)S(1)}, bf16[256,128]{1,0:T(8,128)(2,1)S(1)}, bf16[256,128]{1,0:T(8,128)(2,1)S(1)}, f32[128,128]{1,0:T(8,128)S(1...) custom-call(bf16[256,2048]{1,0:T(8,128)(2,1)S(1)} %copy-done.2, ...), custom_call_target="tpu_custom_call" | custom-call | flops 1500000000 | bytes 10000000 | tf_op jit(solution)/shard_map/project/pallas_call | solution.py:374
  10.5 0.0 collective-permute-done.w_sib
  10.5 0.0 copy-done
  10.5 7.2 %attend_32.1 = (f32[48,2048]{1,0:T(8,128)S(1)}, f32[48,2048]{1,0:T(8,128)}) custom-call(s32[8,128]{1,0:T(8,128)S(1)} %get-tuple-element.17.meta._order, bf16[8,128,128]{2,1,0:T(8,128)(2,1)S(1)} %get-tuple-element.18.q_ref, f32[128,128]{1,0:T(8,128)S(1)} %get-tuple-element.19.kp, f32[128,128]{1,0:T(8,128)S(1)} %get-tuple-element.20.vp, ...), custom_call_target="tpu_custom_call" | custom-call | flops 1200000000 | bytes 8000000 | tf_op jit(solution)/shard_map/attend_32/pallas_call | solution.py:347
  17.8 2.7 %collective-permute-start.1 = (f32[48,2048]{1,0:T(8,128)}, f32[48,2048]{1,0:T(8,128)}, u32[]{:S(2)}, u32[]{:S(2)}) collective-permute-start(f32[48,2048]{1,0:T(8,128)} %get-tuple-element.23), channel_id=1, source_target_pairs={{0,2},{1,3},{2,0},{3,1},{4,6},{5,7},{6,4},{7,5}} | collective-permute-start | bytes 1179656 | tf_op jit(solution)/shard_map/ppermute | solution.py:400
  20.5 13.4 %attend_0.1 = (f32[16,2048]{1,0:T(8,128)S(1)}, f32[16,2048]{1,0:T(8,128)S(1)}) custom-call(s32[8,128]{1,0:T(8,128)S(1)} %get-tuple-element.17.meta._order, bf16[8,128,128]{2,1,0:T(8,128)(2,1)S(1)} %get-tuple-element.18.q_ref, f32[128,128]{1,0:T(8,128)S(1)} %get-tuple-element.19.kp, f32[128,128]{1,0:T(8,128)S(1)} %get-tuple-element.20.vp, ...), custom_call_target="tpu_custom_call" | custom-call | flops 3000000000 | bytes 20000000 | tf_op jit(solution)/shard_map/attend_0/pallas_call | solution.py:347
  33.9 0.0 collective-permute-done.1.r1
  33.9 0.0 copy-done.3
  33.9 11.9 %combine.1 = bf16[256,2048]{1,0:T(8,128)(2,1)S(1)} custom-call(f32[48,2048]{1,0:T(8,128)S(1)} %get-tuple-element.22._order.p1, f32[48,2048]{1,0:T(8,128)} %collective-permute-done.1.r1, f32[16,2048]{1,0:T(8,128)S(1)} %get-tuple-element.24.p2, f32[16,2048]{1,0:T(8,128)S(1)} %get-tuple-element.25.s2, bf16[256,2048]{1,0:T(8,128)(2,1)S(1)} %copy-done.3, ...), custom_call_target="tpu_custom_call" | custom-call | flops 3000000000 | bytes 20000000 | tf_op jit(solution)/shard_map/combine/pallas_call | solution.py:402
  45.8 1.4 %convolution_convert_fusion = bf16[256,2048]{1,0:T(8,128)(2,1)} fusion(bf16[256,256]{1,0:T(8,128)(2,1)S(1)} %get-tuple-element.16, bf16[256,2048]{1,0:T(8,128)(2,1)S(1)} %combine.1), kind=kOutput, calls=%fused_computation | convolution fusion | flops 268959744 | bytes 2228224 | tf_op jit(solution)/shard_map/dot_general | solution.py:417
  47.2 0.6 %copy.13 = bf16[256,1,128]{2,0,1:T(8,128)(2,1)} copy(bf16[256,1,128]{2,0,1:T(8,128)(2,1)S(1)} %bitcast.6) | data formatting | bytes 131072
  47.8 0.6 %copy.14 = bf16[256,1,128]{2,0,1:T(8,128)(2,1)} copy(bf16[256,1,128]{2,0,1:T(8,128)(2,1)S(1)} %bitcast.5) | data formatting | bytes 131072
  (1 shorter events, 0.0 us)
Async XLA Ops:
  0.6 9.9 %collective-permute-start = (bf16[512,2048]{1,0:T(8,128)(2,1)}, bf16[512,2048]{1,0:T(8,128)(2,1)S(1)}, u32[]{:S(2)}, u32[]{:S(2)}) collective-permute-start(bf16[512,2048]{1,0:T(8,128)(2,1)} %w_own.3), channel_id=1, source_target_pairs={{0,1},{1,0},{2,3},{3,2},{4,5},{5,4},{6,7},{7,6}} | collective-permute-start | bytes 6291464 | tf_op jit(solution)/shard_map/ppermute | solution.py:373
  1.5 1.6 %copy-start.1 = (bf16[2048,512]{1,0:T(8,128)(2,1)S(1)}, bf16[2048,512]{1,0:T(8,128)(2,1)}, u32[]{:S(2)}) copy-start(bf16[2048,512]{1,0:T(8,128)(2,1)} %wq_hbm.1) | copy-start | bytes 6291460
  3.1 1.2 %copy-start.2 = (bf16[256,2048]{1,0:T(8,128)(2,1)S(1)}, bf16[256,2048]{1,0:T(8,128)(2,1)}, u32[]{:S(2)}) copy-start(bf16[256,2048]{1,0:T(8,128)(2,1)} %x_ref.1) | copy-start | bytes 3145732
  4.3 1.0 %copy-start.4 = (bf16[2048,128]{1,0:T(8,128)(2,1)S(1)}, bf16[2048,128]{1,0:T(8,128)(2,1)}, u32[]{:S(2)}) copy-start(bf16[2048,128]{1,0:T(8,128)(2,1)} %wk_hbm.1) | copy-start | bytes 1572868
  5.4 1.0 %copy-start.5 = (bf16[2048,128]{1,0:T(8,128)(2,1)S(1)}, bf16[2048,128]{1,0:T(8,128)(2,1)}, u32[]{:S(2)}) copy-start(bf16[2048,128]{1,0:T(8,128)(2,1)} %wv_hbm.1) | copy-start | bytes 1572868
  6.4 0.7 %copy-start.6 = (s32[256]{0:T(256)S(1)}, s32[256]{0:T(256)}, u32[]{:S(2)}) copy-start(s32[256]{0:T(256)} %param.15) | copy-start | bytes 3076
  7.1 3.4 %copy-start = (bf16[512,2048]{1,0:T(8,128)(2,1)S(1)}, bf16[512,2048]{1,0:T(8,128)(2,1)}, u32[]{:S(2)}) copy-start(bf16[512,2048]{1,0:T(8,128)(2,1)} %w_own.3) | copy-start | bytes 6291460
  17.8 16.1 %collective-permute-start.1 = (f32[48,2048]{1,0:T(8,128)}, f32[48,2048]{1,0:T(8,128)}, u32[]{:S(2)}, u32[]{:S(2)}) collective-permute-start(f32[48,2048]{1,0:T(8,128)} %get-tuple-element.23), channel_id=1, source_target_pairs={{0,2},{1,3},{2,0},{3,1},{4,6},{5,7},{6,4},{7,5}} | collective-permute-start | bytes 1179656 | tf_op jit(solution)/shard_map/ppermute | solution.py:400
  20.5 13.4 %copy-start.3 = (bf16[256,2048]{1,0:T(8,128)(2,1)S(1)}, bf16[256,2048]{1,0:T(8,128)(2,1)}, u32[]{:S(2)}) copy-start(bf16[256,2048]{1,0:T(8,128)(2,1)} %x_ref.1) | copy-start | bytes 3145732
